TPU v7x, 32 devices: a whole 2x2x4 slice. The times are simulated.
32 devices in a mesh: ha: 2 (over x), vert: 16 (over z, y, core).
Axes of the slice: x: 2, y: 2, z: 4, core: 2. Of those that a mesh axis runs over, the one named last changes fastest.
Arguments:
- hidden: bfloat16 [128, 16384], P('vert', 'ha'), may hold values from -6 to 6
- norm_gain: float32 [16384], P('ha'), may hold values from 0.25 to 1.75
- head_weight: bfloat16 [16384, 32064], P('ha', 'vert'), may hold values from -0.046875 to 0.046875
- targets: int32 [128], replicated, may hold values from 0 to 32063
Outputs:
- log_probs: float32 [128, 32064], P('ha', 'vert')
- target_logprob: float32 [128], P('ha')
Inputs may be any that keep to these rules, and one draw needn't show every extreme that they name: `targets`: every next token id lies in 0 to 32063.
All inputs are finite; a program needn't handle non-finite values.
Results may differ from a plain program's by a relative error of at most 0.0015.
Values may be sent and summed in bfloat16 or wider, within the bound.
A program may use at most 64 MiB of HBM per device.

v0:
```python
import jax
import jax.numpy as jnp
from jax import lax
from jax.sharding import PartitionSpec as P

D = 16384


def combined_all(part, axis, combine):
    gathered = jax.tree.map(lambda a: lax.all_gather(a, axis), part)

    def take(source):
        return jax.tree.map(lambda a: lax.dynamic_index_in_dim(a, source, 0, False), gathered)

    return lax.fori_loop(
        1, lax.axis_size(axis), lambda source, state: combine(state, take(source)), take(0)
    )


def combine(earlier, later_one):
    largest = jnp.maximum(earlier[0], later_one[0])
    expsum = earlier[1] * jnp.exp(earlier[0] - largest) + later_one[1] * jnp.exp(
        later_one[0] - largest
    )
    return (largest, expsum, earlier[2] + later_one[2])


def shards(hidden, norm_gain, head_weight, targets):
    vocab_width = head_weight.shape[1]
    vocab_start = lax.axis_index("vert") * vocab_width
    ha_count = lax.axis_size("ha")
    batch_total = hidden.shape[0] * lax.axis_size("vert")
    own_rows = batch_total // ha_count

    def partial_terms(block_rows):
        widened = block_rows.astype(jnp.float32)
        scaled = (widened * norm_gain[None, :]).astype(jnp.bfloat16)
        product = jnp.dot(scaled, head_weight, preferred_element_type=jnp.float32)
        squares = jnp.sum(widened * widened, axis=1, keepdims=True)
        return jnp.concatenate([product, squares], axis=1)

    def finish(summed, row_targets):
        unscaled = summed[:, :vocab_width]
        inverse = lax.rsqrt(summed[:, vocab_width:] / D + 1e-05)
        logits = unscaled * inverse
        local_max = jnp.max(logits, axis=1)
        local_sum = jnp.sum(jnp.exp(logits - local_max[:, None]), axis=1)
        columns = vocab_start + jnp.arange(vocab_width, dtype=jnp.int32)
        matches = row_targets[:, None] == columns[None, :]
        local_target = jnp.sum(jnp.where(matches, logits, 0.0), axis=1)
        largest, expsum, target_sum = combined_all(
            (local_max, local_sum, local_target), "vert", combine
        )
        log_total = largest + jnp.log(expsum)
        return (logits - log_total[:, None], target_sum - log_total)

    first_row = lax.axis_index("ha") * own_rows
    gathered = lax.all_gather(hidden, "vert", axis=0, tiled=True)
    summed = lax.psum_scatter(
        partial_terms(lax.slice_in_dim(gathered, 0, own_rows * lax.axis_size("ha"), axis=0)).astype(
            jnp.bfloat16
        ),
        "ha",
        scatter_dimension=0,
        tiled=True,
    ).astype(jnp.float32)
    row_targets = lax.dynamic_slice_in_dim(targets, first_row, own_rows, 0)
    log_probs, picked = finish(summed, row_targets)
    return (log_probs, picked)


def solution(mesh):
    placed = (P("vert", "ha"), P("ha"), P("ha", "vert"), P())
    return jax.shard_map(
        shards, mesh=mesh, in_specs=placed, out_specs=(P("ha", "vert"), P("ha")), check_vma=False
    )
```

profile of v0, /device:TPU:0, one launch (start us, length us, event | category | flops | bytes accessed | tf_op | source)
XLA Modules:
  0.0 159.8 jit_solution(11805804333639017836)
XLA Ops:
  7.2 0.7 all-gather.5.cloned.1.call-update
  7.9 0.0 reduce-scatter.4.cloned.1.call-start
  7.9 46.4 %all-gather.5.cloned.1.call-done = bf16[128,8192]{1,0:T(8,128)(2,1)} async-done(((bf16[8,8192]{1,0:T(8,128)(2,1)}), bf16[128,8192]{1,0:T(8,128)(2,1)}) %all-gather.5.cloned.1.call-update) | async-done | bytes 2097168 | tf_op jit(solution)/shard_map/all_gather | solution.py:58
  54.4 2.1 %fusion.8 = bf16[128]{0:T(256)(128)(2,1)S(1)} fusion(bf16[128,8192]{1,0:T(8,128)(2,1)} %all-gather.5.cloned.1.call-done), kind=kLoop, calls=%fused_computation.13 | loop fusion | flops 3145600 | bytes 2097408 | tf_op jit(solution)/shard_map/reduce_sum | solution.py:39
  56.5 14.9 %convolution_convert_fusion = bf16[128,2004]{0,1:T(8,128)(2,1)S(1)} fusion(bf16[8192,2004]{0,1:T(8,128)(2,1)} %param.8, bf16[128,8192]{1,0:T(8,128)(2,1)} %all-gather.5.cloned.1.call-done, f32[8192]{0:T(1024)} %param.7), kind=kOutput, calls=%fused_computation.14 | convolution fusion | flops 4206094848 | bytes 35476480 | tf_op jit(solution)/shard_map/dot_general | solution.py:38
  71.4 1.0 copy.8
  72.5 0.1 dynamic_slice.45
  72.6 0.6 dynamic-slice
  73.9 12.1 %reduce-scatter.4.cloned.1.call-done = bf16[64,2005]{1,0:T(8,128)(2,1)} async-done(((bf16[128,2005]{1,0:T(8,128)(2,1)}), bf16[64,2005]{1,0:T(8,128)(2,1)}) %reduce-scatter.4.cloned.1.call-update) | async-done | bytes 256656
  86.0 1.2 copy.9
  87.3 0.1 convert_element_type.12
  87.4 0.3 fusion.12
  87.6 1.0 select_reduce_fusion
  88.6 0.2 dynamic-update-slice
  88.9 0.2 dynamic-update-slice.2
  89.1 0.2 dynamic-update-slice.1
  89.3 61.0 %all-reduce.3 = (f32[1024]{0:T(1024)S(1)}, f32[1024]{0:T(1024)S(1)}, f32[1024]{0:T(1024)S(1)}) all-reduce(f32[1024]{0:T(1024)S(1)} %dynamic-update-slice, f32[1024]{0:T(1024)S(1)} %dynamic-update-slice.1, f32[1024]{0:T(1024)S(1)} %dynamic-update-slice.2), channel_id=2, replica_groups=mesh['ha'=2,'vert'=16] {'vert'}, use_global_device_ids=true, to_apply=%add | all-reduce | flops 3072 | bytes 24576
  150.3 0.1 reshape.12
  150.4 0.1 reshape.13
  150.4 0.1 reshape.14
  150.5 0.7 while.19
  151.2 0.5 fusion.17
  151.7 0.1 fusion.11
  151.8 1.1 copy.7
  (30 shorter events, 0.6 us)
Async XLA Ops:
  7.2 47.2 %all-gather.5.cloned.1.call-start = ((), (), s32[]{:S(2)}) async-start(), calls=%async_computation.1 | async-start | bytes 2228224 | tf_op jit(solution)/shard_map/all_gather | solution.py:58
  7.9 78.1 %reduce-scatter.4.cloned.1.call-start = ((), (), s32[]{:S(2)}) async-start(), calls=%async_computation.2 | async-start | bytes 786432
  56.4 16.1 %copy-start = (s32[128]{0:T(128)S(1)}, s32[128]{0:T(128)}, u32[]{:S(2)}) copy-start(s32[128]{0:T(128)} %param.9) | copy-start | bytes 1540
  56.4 16.2 %copy-start.1 = (u32[32]{0:T(128)S(1)}, u32[32]{0:T(128)}, u32[]{:S(2)}) copy-start(u32[32]{0:T(128)} %constant.79) | copy-start | bytes 388
Sparse Core Ops, SparseCore 0:
  10.1 44.1 all-gather.4
  72.6 13.3 reduce-scatter.3
where the time goes:
time: 160 us
  blocking collectives  61 us (38%)
  waiting for transfers between devices  59.2 us (37%)
  matrix products  14.9 us (9%)
  between operations  14.8 us (9%)
  local copies, waits for them, and re-layouts  5.02 us (3%)
  other arithmetic  4.48 us (3%)
    unnamed x1, blocking collectives  61 us
    all_gather x1, waiting for transfers between devices, shards(): gathered = lax.all_gather(hidden, 'vert', axis=0, tiled=True)  46.4 us
    dot_general x1, matrix products, partial_terms(): product = jnp.dot(scaled, head_weight, preferred_element_type=jnp.float32)  14.9 us
    unnamed x3, waiting for transfers between devices  12.8 us
    unnamed x14, local copies, waits for them, and re-layouts  4.73 us
  transfers between devices with their start and end apart: 2, of which 2 were waited for; matrix products, arithmetic and copies ran while one was open for 0% of the time, Pallas kernels for 0%

commit v1 on v0

--- a/solution.py
+++ b/solution.py
@@ -55,7 +55,12 @@
         return (logits - log_total[:, None], target_sum - log_total)
 
     first_row = lax.axis_index("ha") * own_rows
-    gathered = lax.all_gather(hidden, "vert", axis=0, tiled=True)
+    ring = [hidden]
+    for hop in range(15):
+        ring.append(lax.ppermute(ring[-1], "vert", [(dev, (dev + 1) % 16) for dev in range(16)]))
+    gathered = jnp.roll(
+        jnp.concatenate(ring[::-1], axis=0), (lax.axis_index("vert") + 1) * ring[0].shape[0], axis=0
+    )
     summed = lax.psum_scatter(
         partial_terms(lax.slice_in_dim(gathered, 0, own_rows * lax.axis_size("ha"), axis=0)).astype(
             jnp.bfloat16

time: 160 us -> 219 us (1.37)
  waiting for transfers between devices: 59.2 us -> 118 us
    ppermute x0 -> x15, waiting for transfers between devices: none -> 107 us  [shards(): lax.ppermute(ring[-1], 'vert', [(dev, (dev + 1) % 16) for dev in range(16)])]
    all_gather x1 -> x0, waiting for transfers between devices: 46.4 us -> none  [shards(): gathered = lax.all_gather(hidden, 'vert', axis=0, tiled=True)]
    unnamed x3 -> x2, waiting for transfers between devices: 12.8 us -> 11 us
    unnamed x14 -> x49, local copies, waits for them, and re-layouts: 4.73 us -> 6.01 us
  transfers between devices with their start and end apart: 2 -> 16, of which waited for: 2 -> 16; matrix products, arithmetic and copies ran while one was open for 0% -> 0% of each run, Pallas kernels for 0% -> 0%
where the time goes in v1:
time: 219 us; the launch traced here: 218 us
  waiting for transfers between devices  118 us (54%)
  blocking collectives  61 us (28%)
  between operations  15.1 us (7%)
  matrix products  14.1 us (6%)
  local copies, waits for them, and re-layouts  6.31 us (3%)
  other arithmetic  2.9 us (1%)
    ppermute x15, waiting for transfers between devices, shards(): lax.ppermute(ring[-1], 'vert', [(dev, (dev + 1) % 16) for dev in range(16)])  107 us
    unnamed x1, blocking collectives  61 us
    dot_general x1, matrix products, partial_terms(): product = jnp.dot(scaled, head_weight, preferred_element_type=jnp.float32)  14.1 us
    unnamed x2, waiting for transfers between devices  11 us
    unnamed x49, local copies, waits for them, and re-layouts  6.01 us
  transfers between devices with their start and end apart: 16, of which 16 were waited for; matrix products, arithmetic and copies ran while one was open for 0% of the time, Pallas kernels for 0%

profile of v1, /device:TPU:0, one launch (start us, length us, event | category | flops | bytes accessed | tf_op | source)
XLA Modules:
  0.0 218.4 jit_solution(3620379497404247836)
XLA Ops:
  7.8 7.8 %collective-permute-done = bf16[8,8192]{1,0:T(8,128)(2,1)S(1)} collective-permute-done((bf16[8,8192]{1,0:T(8,128)(2,1)}, bf16[8,8192]{1,0:T(8,128)(2,1)S(1)}, u32[]{:S(2)}, u32[]{:S(2)}) %collective-permute-start) | collective-permute-done | bytes 131104 | tf_op jit(solution)/shard_map/ppermute | solution.py:60
  15.6 7.1 %collective-permute-done.1 = bf16[8,8192]{1,0:T(8,128)(2,1)S(1)} collective-permute-done((bf16[8,8192]{1,0:T(8,128)(2,1)S(1)}, bf16[8,8192]{1,0:T(8,128)(2,1)S(1)}, u32[]{:S(2)}, u32[]{:S(2)}) %collective-permute-start.1) | collective-permute-done | bytes 131104 | tf_op jit(solution)/shard_map/ppermute | solution.py:60
  22.7 7.1 %collective-permute-done.2 = bf16[8,8192]{1,0:T(8,128)(2,1)S(1)} collective-permute-done((bf16[8,8192]{1,0:T(8,128)(2,1)S(1)}, bf16[8,8192]{1,0:T(8,128)(2,1)S(1)}, u32[]{:S(2)}, u32[]{:S(2)}) %collective-permute-start.2) | collective-permute-done | bytes 131104 | tf_op jit(solution)/shard_map/ppermute | solution.py:60
  29.8 7.1 %collective-permute-done.3 = bf16[8,8192]{1,0:T(8,128)(2,1)S(1)} collective-permute-done((bf16[8,8192]{1,0:T(8,128)(2,1)S(1)}, bf16[8,8192]{1,0:T(8,128)(2,1)S(1)}, u32[]{:S(2)}, u32[]{:S(2)}) %collective-permute-start.3) | collective-permute-done | bytes 131104 | tf_op jit(solution)/shard_map/ppermute | solution.py:60
  36.9 7.1 %collective-permute-done.4 = bf16[8,8192]{1,0:T(8,128)(2,1)S(1)} collective-permute-done((bf16[8,8192]{1,0:T(8,128)(2,1)S(1)}, bf16[8,8192]{1,0:T(8,128)(2,1)S(1)}, u32[]{:S(2)}, u32[]{:S(2)}) %collective-permute-start.4) | collective-permute-done | bytes 131104 | tf_op jit(solution)/shard_map/ppermute | solution.py:60
  44.0 7.1 %collective-permute-done.5 = bf16[8,8192]{1,0:T(8,128)(2,1)S(1)} collective-permute-done((bf16[8,8192]{1,0:T(8,128)(2,1)S(1)}, bf16[8,8192]{1,0:T(8,128)(2,1)S(1)}, u32[]{:S(2)}, u32[]{:S(2)}) %collective-permute-start.5) | collective-permute-done | bytes 131104 | tf_op jit(solution)/shard_map/ppermute | solution.py:60
  51.1 7.1 %collective-permute-done.6 = bf16[8,8192]{1,0:T(8,128)(2,1)S(1)} collective-permute-done((bf16[8,8192]{1,0:T(8,128)(2,1)S(1)}, bf16[8,8192]{1,0:T(8,128)(2,1)S(1)}, u32[]{:S(2)}, u32[]{:S(2)}) %collective-permute-start.6) | collective-permute-done | bytes 131104 | tf_op jit(solution)/shard_map/ppermute | solution.py:60
  58.2 7.1 %collective-permute-done.7 = bf16[8,8192]{1,0:T(8,128)(2,1)S(1)} collective-permute-done((bf16[8,8192]{1,0:T(8,128)(2,1)S(1)}, bf16[8,8192]{1,0:T(8,128)(2,1)S(1)}, u32[]{:S(2)}, u32[]{:S(2)}) %collective-permute-start.7) | collective-permute-done | bytes 131104 | tf_op jit(solution)/shard_map/ppermute | solution.py:60
  65.2 7.1 %collective-permute-done.8 = bf16[8,8192]{1,0:T(8,128)(2,1)S(1)} collective-permute-done((bf16[8,8192]{1,0:T(8,128)(2,1)S(1)}, bf16[8,8192]{1,0:T(8,128)(2,1)S(1)}, u32[]{:S(2)}, u32[]{:S(2)}) %collective-permute-start.8) | collective-permute-done | bytes 131104 | tf_op jit(solution)/shard_map/ppermute | solution.py:60
  72.3 7.1 %collective-permute-done.9 = bf16[8,8192]{1,0:T(8,128)(2,1)S(1)} collective-permute-done((bf16[8,8192]{1,0:T(8,128)(2,1)S(1)}, bf16[8,8192]{1,0:T(8,128)(2,1)S(1)}, u32[]{:S(2)}, u32[]{:S(2)}) %collective-permute-start.9) | collective-permute-done | bytes 131104 | tf_op jit(solution)/shard_map/ppermute | solution.py:60
  79.4 7.1 %collective-permute-done.10 = bf16[8,8192]{1,0:T(8,128)(2,1)S(1)} collective-permute-done((bf16[8,8192]{1,0:T(8,128)(2,1)S(1)}, bf16[8,8192]{1,0:T(8,128)(2,1)S(1)}, u32[]{:S(2)}, u32[]{:S(2)}) %collective-permute-start.10) | collective-permute-done | bytes 131104 | tf_op jit(solution)/shard_map/ppermute | solution.py:60
  86.5 7.1 %collective-permute-done.11 = bf16[8,8192]{1,0:T(8,128)(2,1)S(1)} collective-permute-done((bf16[8,8192]{1,0:T(8,128)(2,1)S(1)}, bf16[8,8192]{1,0:T(8,128)(2,1)S(1)}, u32[]{:S(2)}, u32[]{:S(2)}) %collective-permute-start.11) | collective-permute-done | bytes 131104 | tf_op jit(solution)/shard_map/ppermute | solution.py:60
  93.6 7.1 %collective-permute-done.12 = bf16[8,8192]{1,0:T(8,128)(2,1)S(1)} collective-permute-done((bf16[8,8192]{1,0:T(8,128)(2,1)S(1)}, bf16[8,8192]{1,0:T(8,128)(2,1)S(1)}, u32[]{:S(2)}, u32[]{:S(2)}) %collective-permute-start.12) | collective-permute-done | bytes 131104 | tf_op jit(solution)/shard_map/ppermute | solution.py:60
  100.7 7.1 %collective-permute-done.13 = bf16[8,8192]{1,0:T(8,128)(2,1)S(1)} collective-permute-done((bf16[8,8192]{1,0:T(8,128)(2,1)S(1)}, bf16[8,8192]{1,0:T(8,128)(2,1)S(1)}, u32[]{:S(2)}, u32[]{:S(2)}) %collective-permute-start.13) | collective-permute-done | bytes 131104 | tf_op jit(solution)/shard_map/ppermute | solution.py:60
  107.8 7.1 %collective-permute-done.14 = bf16[8,8192]{1,0:T(8,128)(2,1)S(1)} collective-permute-done((bf16[8,8192]{1,0:T(8,128)(2,1)S(1)}, bf16[8,8192]{1,0:T(8,128)(2,1)S(1)}, u32[]{:S(2)}, u32[]{:S(2)}) %collective-permute-start.14) | collective-permute-done | bytes 131104 | tf_op jit(solution)/shard_map/ppermute | solution.py:60
  115.2 0.9 constant_dynamic-update-slice_fusion.16
  116.9 14.1 %convolution_convert_fusion = bf16[128,2004]{0,1:T(8,128)(2,1)S(1)} fusion(bf16[8192,2004]{0,1:T(8,128)(2,1)} %param.8, f32[8192]{0:T(1024)S(1)} %copy-done.1, bf16[256,8192]{1,0:T(8,128)(2,1)S(1)} %constant_dynamic-update-slice_fusion, s32[]{:T(128)S(6)} %select_n.37), kind=kOutput, calls=%fused_computation.14 | convolution fusion | flops 4206094848 | bytes 35476484 | tf_op jit(solution)/shard_map/dot_general | solution.py:38
  131.0 1.0 copy.8
  133.6 11.0 %reduce-scatter.4.cloned.1.call-done = bf16[64,2005]{1,0:T(8,128)(2,1)} async-done(((bf16[128,2005]{1,0:T(8,128)(2,1)}), bf16[64,2005]{1,0:T(8,128)(2,1)}) %reduce-scatter.4.cloned.1.call-update) | async-done | bytes 256656
  144.6 1.2 copy.9
  146.2 1.0 select_reduce_fusion
  147.9 61.0 %all-reduce.3 = (f32[1024]{0:T(1024)S(1)}, f32[1024]{0:T(1024)S(1)}, f32[1024]{0:T(1024)S(1)}) all-reduce(f32[1024]{0:T(1024)S(1)} %dynamic-update-slice, f32[1024]{0:T(1024)S(1)} %dynamic-update-slice.1, f32[1024]{0:T(1024)S(1)} %dynamic-update-slice.2), channel_id=2, replica_groups=mesh['ha'=2,'vert'=16] {'vert'}, use_global_device_ids=true, to_apply=%add | all-reduce | flops 3072 | bytes 24576
  209.1 0.7 while.19
  210.4 1.1 copy.7
  (93 shorter events, 4.6 us)
Async XLA Ops:
  7.2 109.2 %copy-start = (bf16[8,8192]{1,0:T(8,128)(2,1)S(1)}, bf16[8,8192]{1,0:T(8,128)(2,1)}, u32[]{:S(2)}) copy-start(bf16[8,8192]{1,0:T(8,128)(2,1)} %param.6) | copy-start | bytes 393220
  7.2 137.4 %reduce-scatter.4.cloned.1.call-start = ((), (), s32[]{:S(2)}) async-start(), calls=%async_computation.1 | async-start | bytes 786432
  7.2 8.4 %collective-permute-start = (bf16[8,8192]{1,0:T(8,128)(2,1)}, bf16[8,8192]{1,0:T(8,128)(2,1)S(1)}, u32[]{:S(2)}, u32[]{:S(2)}) collective-permute-start(bf16[8,8192]{1,0:T(8,128)(2,1)} %param.6), channel_id=1, source_target_pairs={{0,1},{1,2},{2,3},{3,4},{4,5},{5,6},{6,7},{7,8},{8,9},{9,10},{10,1... | collective-permute-start | bytes 393224 | tf_op jit(solution)/shard_map/ppermute | solution.py:60
  15.6 7.1 %collective-permute-start.1 = (bf16[8,8192]{1,0:T(8,128)(2,1)S(1)}, bf16[8,8192]{1,0:T(8,128)(2,1)S(1)}, u32[]{:S(2)}, u32[]{:S(2)}) collective-permute-start(bf16[8,8192]{1,0:T(8,128)(2,1)S(1)} %collective-permute-done), channel_id=1, source_target_pairs={{0,1},{1,2},{2,3},{3,4},{4,5},{5,6},{6,7},{7,8},{8,9},{9,10},{10,1... | collective-permute-start | bytes 393224 | tf_op jit(solution)/shard_map/ppermute | solution.py:60
  22.7 7.1 %collective-permute-start.2 = (bf16[8,8192]{1,0:T(8,128)(2,1)S(1)}, bf16[8,8192]{1,0:T(8,128)(2,1)S(1)}, u32[]{:S(2)}, u32[]{:S(2)}) collective-permute-start(bf16[8,8192]{1,0:T(8,128)(2,1)S(1)} %collective-permute-done.1), channel_id=1, source_target_pairs={{0,1},{1,2},{2,3},{3,4},{4,5},{5,6},{6,7},{7,8},{8,9},{9,10},{10,1... | collective-permute-start | bytes 393224 | tf_op jit(solution)/shard_map/ppermute | solution.py:60
  29.8 7.1 %collective-permute-start.3 = (bf16[8,8192]{1,0:T(8,128)(2,1)S(1)}, bf16[8,8192]{1,0:T(8,128)(2,1)S(1)}, u32[]{:S(2)}, u32[]{:S(2)}) collective-permute-start(bf16[8,8192]{1,0:T(8,128)(2,1)S(1)} %collective-permute-done.2), channel_id=1, source_target_pairs={{0,1},{1,2},{2,3},{3,4},{4,5},{5,6},{6,7},{7,8},{8,9},{9,10},{10,1... | collective-permute-start | bytes 393224 | tf_op jit(solution)/shard_map/ppermute | solution.py:60
  36.9 7.1 %collective-permute-start.4 = (bf16[8,8192]{1,0:T(8,128)(2,1)S(1)}, bf16[8,8192]{1,0:T(8,128)(2,1)S(1)}, u32[]{:S(2)}, u32[]{:S(2)}) collective-permute-start(bf16[8,8192]{1,0:T(8,128)(2,1)S(1)} %collective-permute-done.3), channel_id=1, source_target_pairs={{0,1},{1,2},{2,3},{3,4},{4,5},{5,6},{6,7},{7,8},{8,9},{9,10},{10,1... | collective-permute-start | bytes 393224 | tf_op jit(solution)/shard_map/ppermute | solution.py:60
  44.0 7.1 %collective-permute-start.5 = (bf16[8,8192]{1,0:T(8,128)(2,1)S(1)}, bf16[8,8192]{1,0:T(8,128)(2,1)S(1)}, u32[]{:S(2)}, u32[]{:S(2)}) collective-permute-start(bf16[8,8192]{1,0:T(8,128)(2,1)S(1)} %collective-permute-done.4), channel_id=1, source_target_pairs={{0,1},{1,2},{2,3},{3,4},{4,5},{5,6},{6,7},{7,8},{8,9},{9,10},{10,1... | collective-permute-start | bytes 393224 | tf_op jit(solution)/shard_map/ppermute | solution.py:60
  51.1 7.1 %collective-permute-start.6 = (bf16[8,8192]{1,0:T(8,128)(2,1)S(1)}, bf16[8,8192]{1,0:T(8,128)(2,1)S(1)}, u32[]{:S(2)}, u32[]{:S(2)}) collective-permute-start(bf16[8,8192]{1,0:T(8,128)(2,1)S(1)} %collective-permute-done.5), channel_id=1, source_target_pairs={{0,1},{1,2},{2,3},{3,4},{4,5},{5,6},{6,7},{7,8},{8,9},{9,10},{10,1... | collective-permute-start | bytes 393224 | tf_op jit(solution)/shard_map/ppermute | solution.py:60
  58.2 7.1 %collective-permute-start.7 = (bf16[8,8192]{1,0:T(8,128)(2,1)S(1)}, bf16[8,8192]{1,0:T(8,128)(2,1)S(1)}, u32[]{:S(2)}, u32[]{:S(2)}) collective-permute-start(bf16[8,8192]{1,0:T(8,128)(2,1)S(1)} %collective-permute-done.6), channel_id=1, source_target_pairs={{0,1},{1,2},{2,3},{3,4},{4,5},{5,6},{6,7},{7,8},{8,9},{9,10},{10,1... | collective-permute-start | bytes 393224 | tf_op jit(solution)/shard_map/ppermute | solution.py:60
  65.2 7.1 %collective-permute-start.8 = (bf16[8,8192]{1,0:T(8,128)(2,1)S(1)}, bf16[8,8192]{1,0:T(8,128)(2,1)S(1)}, u32[]{:S(2)}, u32[]{:S(2)}) collective-permute-start(bf16[8,8192]{1,0:T(8,128)(2,1)S(1)} %collective-permute-done.7), channel_id=1, source_target_pairs={{0,1},{1,2},{2,3},{3,4},{4,5},{5,6},{6,7},{7,8},{8,9},{9,10},{10,1... | collective-permute-start | bytes 393224 | tf_op jit(solution)/shard_map/ppermute | solution.py:60
  72.3 7.1 %collective-permute-start.9 = (bf16[8,8192]{1,0:T(8,128)(2,1)S(1)}, bf16[8,8192]{1,0:T(8,128)(2,1)S(1)}, u32[]{:S(2)}, u32[]{:S(2)}) collective-permute-start(bf16[8,8192]{1,0:T(8,128)(2,1)S(1)} %collective-permute-done.8), channel_id=1, source_target_pairs={{0,1},{1,2},{2,3},{3,4},{4,5},{5,6},{6,7},{7,8},{8,9},{9,10},{10,1... | collective-permute-start | bytes 393224 | tf_op jit(solution)/shard_map/ppermute | solution.py:60
  79.4 7.1 %collective-permute-start.10 = (bf16[8,8192]{1,0:T(8,128)(2,1)S(1)}, bf16[8,8192]{1,0:T(8,128)(2,1)S(1)}, u32[]{:S(2)}, u32[]{:S(2)}) collective-permute-start(bf16[8,8192]{1,0:T(8,128)(2,1)S(1)} %collective-permute-done.9), channel_id=1, source_target_pairs={{0,1},{1,2},{2,3},{3,4},{4,5},{5,6},{6,7},{7,8},{8,9},{9,10},{10,1... | collective-permute-start | bytes 393224 | tf_op jit(solution)/shard_map/ppermute | solution.py:60
  86.5 7.1 %collective-permute-start.11 = (bf16[8,8192]{1,0:T(8,128)(2,1)S(1)}, bf16[8,8192]{1,0:T(8,128)(2,1)S(1)}, u32[]{:S(2)}, u32[]{:S(2)}) collective-permute-start(bf16[8,8192]{1,0:T(8,128)(2,1)S(1)} %collective-permute-done.10), channel_id=1, source_target_pairs={{0,1},{1,2},{2,3},{3,4},{4,5},{5,6},{6,7},{7,8},{8,9},{9,10},{10,1... | collective-permute-start | bytes 393224 | tf_op jit(solution)/shard_map/ppermute | solution.py:60
  93.6 7.1 %collective-permute-start.12 = (bf16[8,8192]{1,0:T(8,128)(2,1)S(1)}, bf16[8,8192]{1,0:T(8,128)(2,1)S(1)}, u32[]{:S(2)}, u32[]{:S(2)}) collective-permute-start(bf16[8,8192]{1,0:T(8,128)(2,1)S(1)} %collective-permute-done.11), channel_id=1, source_target_pairs={{0,1},{1,2},{2,3},{3,4},{4,5},{5,6},{6,7},{7,8},{8,9},{9,10},{10,1... | collective-permute-start | bytes 393224 | tf_op jit(solution)/shard_map/ppermute | solution.py:60
  100.7 7.1 %collective-permute-start.13 = (bf16[8,8192]{1,0:T(8,128)(2,1)S(1)}, bf16[8,8192]{1,0:T(8,128)(2,1)S(1)}, u32[]{:S(2)}, u32[]{:S(2)}) collective-permute-start(bf16[8,8192]{1,0:T(8,128)(2,1)S(1)} %collective-permute-done.12), channel_id=1, source_target_pairs={{0,1},{1,2},{2,3},{3,4},{4,5},{5,6},{6,7},{7,8},{8,9},{9,10},{10,1... | collective-permute-start | bytes 393224 | tf_op jit(solution)/shard_map/ppermute | solution.py:60
  107.8 7.1 %collective-permute-start.14 = (bf16[8,8192]{1,0:T(8,128)(2,1)S(1)}, bf16[8,8192]{1,0:T(8,128)(2,1)S(1)}, u32[]{:S(2)}, u32[]{:S(2)}) collective-permute-start(bf16[8,8192]{1,0:T(8,128)(2,1)S(1)} %collective-permute-done.13), channel_id=1, source_target_pairs={{0,1},{1,2},{2,3},{3,4},{4,5},{5,6},{6,7},{7,8},{8,9},{9,10},{10,1... | collective-permute-start | bytes 393224 | tf_op jit(solution)/shard_map/ppermute | solution.py:60
  115.0 1.9 copy-start.1
  116.9 15.2 %copy-start.2 = (s32[128]{0:T(128)S(1)}, s32[128]{0:T(128)}, u32[]{:S(2)}) copy-start(s32[128]{0:T(128)} %param.9) | copy-start | bytes 1540
  116.9 15.3 %copy-start.3 = (u32[32]{0:T(128)S(1)}, u32[32]{0:T(128)}, u32[]{:S(2)}) copy-start(u32[32]{0:T(128)} %constant.102) | copy-start | bytes 388
Sparse Core Ops, SparseCore 0:
  132.2 12.3 reduce-scatter.3
